TPU v7x, 256 devices: a whole 4x4x8 slice. The times are simulated.
256 devices in a mesh: img: 8 (over y, x_lo), cls: 8 (over z), emb: 4 (over x_hi, core).
Axes of the slice: x: 4 (x_hi: 2, x_lo: 2; x = x_hi * 2 + x_lo), y: 4, z: 8, core: 2. Of those that a mesh axis runs over, the one named last changes fastest.
Arguments:
- regions: bfloat16 [8192, 1024], P('img', 'emb'), may hold values from -8 to 8
- table: bfloat16 [21504, 1024], P('cls', 'emb'), may hold values from -1 to 1
- shift: float32 [8192], P('img'), may hold values from -0.5 to 0.1
- scale: float32 [8192], P('img'), may hold values from 2 to 20
- labels: int32 [8192], P('img'), may hold values from -1 to 21503, as said below
- valid: int32 [16, 21504], P('img', 'cls'), may hold values 0 or 1
Outputs:
- loss: float32 [], replicated
- region_grad: bfloat16 [8192, 1024], P('img', 'emb')
- table_grad: bfloat16 [21504, 1024], P('cls', 'emb')
Inputs may be any that keep to these rules, and one draw needn't show every extreme that they name: `labels`: -1 marks background; the first region of every image is foreground.
All inputs are finite; a program needn't handle non-finite values. No bound on the sum of `valid` on one device may be relied on, other than what follows from the above.
Results may differ from a plain program's by a relative error of at most 0.0034.
Values may be sent and summed in bfloat16 or wider, within the bound.
No kernel may reach another device: no remote copies, remote signals or barrier semaphores. Data moves between devices by JAX's collectives and lax.ppermute only.
A program may use at most 64 MiB of HBM per device.

v0:
```python
import functools
import jax
import jax.numpy as jnp
from jax import lax
from jax.sharding import Mesh
from jax.sharding import PartitionSpec as P

CLASSES = 21504
REG_IMG = 512
EMB = ("emb_0", "emb_1")
IMG = ("img_0", "img_1")
IMG_CLS_EMB = ("img_0", "img_1", "cls", "emb_0", "emb_1")


def over_axes(shard, axes):
    return functools.reduce(lax.psum, axes, shard)


def focal(logit, target):
    prob = jax.nn.sigmoid(logit)
    return -0.25 * target * (1.0 - prob) ** 2 * jax.nn.log_sigmoid(logit) - 0.75 * (
        1.0 - target
    ) * prob**2 * jax.nn.log_sigmoid(-logit)


def shards(regions, table, shift, scale, labels, valid):
    rows = regions.shape[0]
    class_dev = table.shape[0]
    parts = lax.axis_size(EMB)
    quarter = rows // parts
    start = lax.axis_index(EMB) * quarter
    block = regions.astype(jnp.float32)
    squares = lax.psum(jnp.sum(block * block, axis=1), EMB)
    local_count = jnp.sum((labels >= 0).astype(jnp.float32))
    count = lax.psum(local_count, IMG)
    inv = lax.rsqrt(squares + 1e-06)
    unit = block * inv[:, None]
    unit_b = unit.astype(jnp.bfloat16)
    unit_rows = lax.all_to_all(unit_b, EMB, split_axis=0, concat_axis=1, tiled=True)
    cosine = lax.dot_general(
        unit_rows,
        lax.all_gather(table, EMB, axis=1, tiled=True),
        (((1,), (1,)), ((), ())),
        preferred_element_type=jnp.float32,
    )
    shift_q = lax.dynamic_slice_in_dim(shift, start, quarter, 0)
    scale_q = lax.dynamic_slice_in_dim(scale, start, quarter, 0)
    label_q = lax.dynamic_slice_in_dim(labels, start, quarter, 0)
    image_ids = (start + jnp.arange(quarter, dtype=jnp.int32)) // REG_IMG
    onehot = (image_ids[:, None] == jnp.arange(valid.shape[0], dtype=jnp.int32)[None, :]).astype(
        jnp.float32
    )
    mask = jnp.dot(onehot, valid.astype(jnp.float32), preferred_element_type=jnp.float32)
    class_ids = lax.axis_index("cls") * class_dev + jnp.arange(class_dev, dtype=jnp.int32)
    logit = (cosine + shift_q[:, None]) * scale_q[:, None]
    target = (label_q[:, None] == class_ids[None, :]).astype(jnp.float32)
    term, pullback = jax.vjp(lambda value: focal(value, target), logit)
    dlogit = pullback(jnp.ones_like(term))[0]
    total = over_axes(jnp.sum(term * mask), IMG_CLS_EMB)
    factor = rows * lax.axis_size(IMG) / count
    dscore = (dlogit * mask * scale_q[:, None] * factor).astype(jnp.bfloat16)
    piece = lax.all_gather(dscore, EMB, axis=0, tiled=True)
    dunit_piece = jnp.dot(piece, table, preferred_element_type=jnp.float32)
    table_acc = lax.dot_general(
        piece, unit_b, (((0,), (0,)), ((), ())), preferred_element_type=jnp.float32
    )
    dunit = lax.psum(dunit_piece, "cls")
    radial = lax.psum(jnp.sum(unit * dunit, axis=1), EMB)
    region_grad = (inv[:, None] * (dunit - unit * radial[:, None])).astype(jnp.bfloat16)
    table_grad = lax.psum(table_acc, IMG).astype(jnp.bfloat16)
    loss = total / count / CLASSES
    return (loss, region_grad, table_grad)


def solution(mesh):
    torus = Mesh(
        mesh.devices.reshape(4, 2, mesh.shape["cls"], 2, 2),
        ("img_0", "img_1", "cls", "emb_0", "emb_1"),
    )
    return jax.shard_map(
        shards,
        mesh=torus,
        in_specs=(P(IMG, EMB), P("cls", EMB), P(IMG), P(IMG), P(IMG), P(IMG, "cls")),
        out_specs=(P(), P(IMG, EMB), P("cls", EMB)),
        check_vma=False,
    )
```

profile of v0, /device:TPU:1, one launch (start us, length us, event | category | flops | bytes accessed | tf_op | source)
XLA Modules:
  0.0 273.6 jit_solution(13197794882755454692)
XLA Ops:
  7.2 0.0 copy-start.2
  7.2 0.0 all-gather.3.cloned.1.call-start
  7.2 0.7 all-gather.3.cloned.1.call-update
  7.9 1.3 fusion.33
  9.2 9.7 %psum.70 = f32[1024]{0:T(1024)S(1)} all-reduce(f32[1024]{0:T(1024)S(1)} %fusion.33), channel_id=1, replica_groups=mesh['img_0'=4,'img_1'=2,'cls'=8,'emb_0'=2,'emb_1'=2] {'emb_0','emb_1'}, use_global_device_ids=true, to_apply=%region_1.0 | all-reduce | flops 1024 | bytes 8192 | tf_op jit(solution)/shard_map/psum | solution.py:33
  18.9 1.2 fusion.28
  20.2 1.0 copy.9
  21.2 5.2 %all-to-all-start = ((bf16[4,256,256]{1,2,0:T(8,128)(2,1)}), bf16[4,256,256]{1,2,0:T(8,128)(2,1)S(1)}, u32[]{:S(2)}, u32[]{:S(2)}) async-start(bf16[4,256,256]{1,2,0:T(8,128)(2,1)} %copy.9), calls=%async_computation | async-start | bytes 1048576 | tf_op jit(solution)/shard_map/all_to_all | solution.py:39
  26.3 0.0 all-gather.5.cloned.1.call-start
  26.3 0.0 copy-done.2
  26.3 0.6 convert_reduce_fusion
  26.9 24.0 %psum.76 = f32[]{:T(128)} all-reduce(f32[]{:T(128)} %convert_reduce_fusion), channel_id=1, replica_groups=mesh['img_0'=4,'img_1'=2,'cls'=8,'emb_0'=2,'emb_1'=2] {'img_0','img_1'}, use_global_device_ids=true, to_apply=%region_9.11 | all-reduce | flops 1 | bytes 8 | tf_op jit(solution)/shard_map/psum | solution.py:35
  51.0 0.1 dynamic_slice.9
  51.0 0.8 dynamic_slice.11
  51.8 0.8 dynamic_slice.10
  53.3 0.0 all-to-all-done
  53.3 15.6 %all-gather.3.cloned.1.call-done = bf16[2688,1024]{1,0:T(8,128)(2,1)} async-done(((bf16[2688,256]{1,0:T(8,128)(2,1)}), bf16[2688,1024]{1,0:T(8,128)(2,1)}) %all-gather.3.cloned.1.call-update) | async-done | bytes 5505040 | tf_op jit(solution)/shard_map/all_gather | solution.py:42
  68.9 0.0 copy-start.3
  68.9 4.5 %fusion = f32[256,2688]{1,0:T(8,128)S(1)} fusion(bf16[256,1024]{0,1:T(8,128)(2,1)S(1)} %bitcast.11, bf16[2688,1024]{1,0:T(8,128)(2,1)} %all-gather.3.cloned.1.call-done, f32[256]{0:T(256)S(1)} %dynamic_slice.11, f32[256]{0:T(256)S(1)} %dynamic_slice.10), kind=kOutput, calls=%fused_computation.7 | convolution fusion | flops 1410662400 | bytes 8783872 | tf_op jit(solution)/shard_map/dot_general | solution.py:40
  73.4 0.0 copy-done.3
  73.4 0.0 copy-start.1
  73.4 9.8 %fusion.12 = (bf16[256,2688]{1,0:T(8,128)(2,1)}, f32[]{:T(128)}) fusion(f32[256,2688]{1,0:T(8,128)S(1)} %fusion, f32[]{:T(128)S(6)} %div.31, f32[256]{0:T(256)S(1)} %dynamic_slice.11, s32[2688]{0:T(1024)S(1)} %iota_add_fusion, s32[256]{0:T(256)S(1)} %dynamic_slice.9, s32[2,2688]{1,0:T(2,128)S(1)} %copy-done.3, s32[256]{0:T(256)S(1)} %and_select_fusion), kind=kOutput, calls=%fused_computation.25 | convolution fusion | flops 47486720 | bytes 4164104 | tf_op jit(solution)/shard_map/dot_general | solution.py:53
  83.2 0.0 all-gather.5.cloned.1.call-update
  83.3 0.0 all-reduce.3.cloned.1.call-start
  83.3 9.4 %psum.71 = f32[]{:T(128)} all-reduce(f32[]{:T(128)} %get-tuple-element.12), channel_id=1, replica_groups=mesh['img_0'=4,'img_1'=2,'cls'=8,'emb_0'=2,'emb_1'=2] {'img_0'}, use_global_device_ids=true, to_apply=%region_3.5 | all-reduce | flops 1 | bytes 8 | tf_op jit(solution)/shard_map/psum | solution.py:16
  92.7 4.4 %psum.72 = f32[]{:T(128)} all-reduce(f32[]{:T(128)} %psum.71), channel_id=1, replica_groups=mesh['img_0'=4,'img_1'=2,'cls'=8,'emb_0'=2,'emb_1'=2] {'img_1'}, use_global_device_ids=true, to_apply=%region_4.6 | all-reduce | flops 1 | bytes 8 | tf_op jit(solution)/shard_map/psum | solution.py:16
  97.1 16.2 %psum.73 = f32[]{:T(128)} all-reduce(f32[]{:T(128)} %psum.72), channel_id=1, replica_groups=mesh['img_0'=4,'img_1'=2,'cls'=8,'emb_0'=2,'emb_1'=2] {'cls'}, use_global_device_ids=true, to_apply=%region_5.7 | all-reduce | flops 1 | bytes 8 | tf_op jit(solution)/shard_map/psum | solution.py:16
  113.3 6.5 %psum.74 = f32[]{:T(128)} all-reduce(f32[]{:T(128)} %psum.73), channel_id=1, replica_groups=mesh['img_0'=4,'img_1'=2,'cls'=8,'emb_0'=2,'emb_1'=2] {'emb_0'}, use_global_device_ids=true, to_apply=%region_6.8 | all-reduce | flops 1 | bytes 8 | tf_op jit(solution)/shard_map/psum | solution.py:16
  119.8 9.1 %psum.75 = f32[]{:T(128)} all-reduce(f32[]{:T(128)} %psum.74), channel_id=1, replica_groups=mesh['img_0'=4,'img_1'=2,'cls'=8,'emb_0'=2,'emb_1'=2] {'emb_1'}, use_global_device_ids=true, to_apply=%region_7.9 | all-reduce | flops 1 | bytes 8 | tf_op jit(solution)/shard_map/psum | solution.py:16
  130.2 1.8 all-gather.5.cloned.1.call-done
  132.0 0.0 copy-done.1
  132.0 5.2 %fusion.37 = f32[1024,256]{1,0:T(8,128)} fusion(bf16[1024,2688]{1,0:T(8,128)(2,1)} %all-gather.5.cloned.1.call-done, bf16[2688,256]{1,0:T(8,128)(2,1)S(1)} %copy-done.1), kind=kOutput, calls=%fused_computation.63 | convolution fusion | flops 1409286144 | bytes 7929856 | tf_op jit(solution)/shard_map/dot_general | solution.py:63
  137.2 0.0 all-reduce.3.cloned.1.call-update
  137.3 4.2 %fusion.38 = f32[2688,256]{1,0:T(8,128)S(1)} fusion(bf16[1024,2688]{1,0:T(8,128)(2,1)} %all-gather.5.cloned.1.call-done, bf16[1024,256]{1,0:T(8,128)(2,1)S(1)} %fusion.28), kind=kOutput, calls=%fused_computation.64 | convolution fusion | flops 1409286144 | bytes 8781824 | tf_op jit(solution)/shard_map/dot_general | solution.py:64
  141.5 0.0 copy-start
  141.5 111.4 %all-reduce.4 = bf16[2688,256]{1,0:T(8,128)(2,1)} all-reduce(f32[2688,256]{1,0:T(8,128)S(1)} %fusion.38), channel_id=1, replica_groups=mesh['img_0'=4,'img_1'=2,'cls'=8,'emb_0'=2,'emb_1'=2] {'img_0','img_1'}, use_global_device_ids=true, to_apply=%region_13.15 | all-reduce | flops 688128 | bytes 4128768 | tf_op jit(solution)/shard_map/psum | solution.py:70
  253.0 0.0 all-reduce.3.cloned.1.call-done
  253.0 0.0 copy-done
  253.0 1.6 fusion.29
  254.6 9.0 %psum.78 = f32[1024]{0:T(1024)S(1)} all-reduce(f32[1024]{0:T(1024)S(1)} %fusion.29), channel_id=1, replica_groups=mesh['img_0'=4,'img_1'=2,'cls'=8,'emb_0'=2,'emb_1'=2] {'emb_0','emb_1'}, use_global_device_ids=true, to_apply=%region_12.14 | all-reduce | flops 1024 | bytes 8192 | tf_op jit(solution)/shard_map/psum | solution.py:68
  263.5 2.4 fusion.32
  (3 shorter events, 0.0 us)
Async XLA Ops:
  7.2 19.2 %copy-start.2 = (s32[1024]{0:T(1024)S(1)}, s32[1024]{0:T(1024)}, u32[]{:S(2)}) copy-start(s32[1024]{0:T(1024)} %param.11) | copy-start | bytes 12292
  7.2 61.7 %all-gather.3.cloned.1.call-start = ((), (), s32[]{:S(2)}) async-start(), calls=%async_computation.1 | async-start | bytes 6881280 | tf_op jit(solution)/shard_map/all_gather | solution.py:42
  21.2 32.1 %all-to-all-start = ((bf16[4,256,256]{1,2,0:T(8,128)(2,1)}), bf16[4,256,256]{1,2,0:T(8,128)(2,1)S(1)}, u32[]{:S(2)}, u32[]{:S(2)}) async-start(bf16[4,256,256]{1,2,0:T(8,128)(2,1)} %copy.9), calls=%async_computation | async-start | bytes 1048576 | tf_op jit(solution)/shard_map/all_to_all | solution.py:39
  26.3 105.7 %all-gather.5.cloned.1.call-start = ((), (), s32[]{:S(2)}) async-start(), calls=%async_computation.2 | async-start | bytes 6881280 | tf_op jit(solution)/shard_map/all_gather | solution.py:62
  68.9 4.5 %copy-start.3 = (s32[2,2688]{1,0:T(2,128)S(1)}, s32[2,2688]{1,0:T(2,128)}, u32[]{:S(2)}) copy-start(s32[2,2688]{1,0:T(2,128)} %param.12) | copy-start | bytes 64516
  73.4 58.6 %copy-start.1 = (bf16[2688,256]{1,0:T(8,128)(2,1)S(1)}, bf16[2688,256]{1,0:T(8,128)(2,1)}, u32[]{:S(2)}) copy-start(bf16[2688,256]{1,0:T(8,128)(2,1)} %param.8) | copy-start | bytes 4128772
  83.3 169.7 %all-reduce.3.cloned.1.call-start = ((), (), s32[]{:S(2)}) async-start(), calls=%async_computation.3 | async-start | bytes 2097152 | tf_op jit(solution)/shard_map/psum | solution.py:67
  141.5 111.5 %copy-start = (bf16[1024,256]{1,0:T(8,128)(2,1)S(1)}, bf16[1024,256]{1,0:T(8,128)(2,1)}, u32[]{:S(2)}) copy-start(bf16[1024,256]{1,0:T(8,128)(2,1)} %param.7) | copy-start | bytes 1572868
Sparse Core Ops, SparseCore 0:
  9.8 59.0 all-gather.2
  83.4 48.5 all-gather.4
  137.4 70.8 all-reduce.2
where the time goes:
time: 274 us
  blocking collectives  200 us (73%)
  matrix products  23.8 us (9%)
  waiting for transfers between devices  18.1 us (7%)
  between operations  17 us (6%)
  other arithmetic  7.09 us (3%)
  starting transfers between devices  5.23 us (2%)
    psum x1, blocking collectives, shards(): table_grad = lax.psum(table_acc, IMG).astype(jnp.bfloat16)  111 us
    psum x5, blocking collectives, over_axes(): return functools.reduce(lax.psum, axes, shard)  45.6 us
    psum x1, blocking collectives, shards(): count = lax.psum(local_count, IMG)  24 us
    all_gather x1, waiting for transfers between devices, shards(): lax.all_gather(table, EMB, axis=1, tiled=True)  15.6 us
    dot_general x1, matrix products, shards(): jnp.dot(onehot, valid.astype(jnp.float32), preferred_element_type=jnp.flo...  9.78 us
    psum x1, blocking collectives, shards(): squares = lax.psum(jnp.sum(block * block, axis=1), EMB)  9.73 us
    psum x1, blocking collectives, shards(): radial = lax.psum(jnp.sum(unit * dunit, axis=1), EMB)  8.96 us
  transfers between devices with their start and end apart: 4, of which 2 were waited for; matrix products, arithmetic and copies ran while one was open for 4% of the time, Pallas kernels for 0%

commit v1 on v0

--- a/solution.py
+++ b/solution.py
@@ -10,6 +10,11 @@
 EMB = ("emb_0", "emb_1")
 IMG = ("img_0", "img_1")
 IMG_CLS_EMB = ("img_0", "img_1", "cls", "emb_0", "emb_1")
+
+
+def by_each_axis(x, axis_one, axis_two):
+    inner = lax.psum(x, axis_one)
+    return lax.psum(inner, axis_two)
 
 
 def over_axes(shard, axes):
@@ -67,7 +72,7 @@
     dunit = lax.psum(dunit_piece, "cls")
     radial = lax.psum(jnp.sum(unit * dunit, axis=1), EMB)
     region_grad = (inv[:, None] * (dunit - unit * radial[:, None])).astype(jnp.bfloat16)
-    table_grad = lax.psum(table_acc, IMG).astype(jnp.bfloat16)
+    table_grad = by_each_axis(table_acc, "img_0", "img_1").astype(jnp.bfloat16)
     loss = total / count / CLASSES
     return (loss, region_grad, table_grad)
 

time: 274 us -> 400 us (1.46)
  waiting for transfers between devices: 18.1 us -> 196 us
  blocking collectives: 200 us -> 146 us
    psum x1 -> x0, blocking collectives: 111 us -> none  [shards(): table_grad = lax.psum(table_acc, IMG).astype(jnp.bfloat16)]
    psum x1, waiting for transfers between devices: 0.01 us -> 74.4 us  [shards(): dunit = lax.psum(dunit_piece, 'cls')]
    psum x0 -> x1, waiting for transfers between devices: none -> 56.9 us  [by_each_axis(): inner = lax.psum(x, axis_one)]
    psum x5, blocking collectives: 45.6 us -> 94.6 us  [over_axes(): return functools.reduce(lax.psum, axes, shard)]
    all_gather x1, waiting for transfers between devices: 1.81 us -> 48.6 us  [shards(): piece = lax.all_gather(dscore, EMB, axis=0, tiled=True)]
    psum x1, blocking collectives: 8.96 us -> 17.2 us  [shards(): radial = lax.psum(jnp.sum(unit * dunit, axis=1), EMB)]
  transfers between devices with their start and end apart: 4 -> 5, of which waited for: 2 -> 4; matrix products, arithmetic and copies ran while one was open for 4% -> 3% of each run, Pallas kernels for 0% -> 0%
where the time goes in v1:
time: 400 us; the launch traced here: 399 us
  waiting for transfers between devices  196 us (49%)
  blocking collectives  146 us (36%)
  matrix products  25.3 us (6%)
  between operations  17 us (4%)
  other arithmetic  5.95 us (1%)
  starting transfers between devices  5.28 us (1%)
    psum x5, blocking collectives, over_axes(): return functools.reduce(lax.psum, axes, shard)  94.6 us
    psum x1, waiting for transfers between devices, shards(): dunit = lax.psum(dunit_piece, 'cls')  74.4 us
    psum x1, waiting for transfers between devices, by_each_axis(): inner = lax.psum(x, axis_one)  56.9 us
    all_gather x1, waiting for transfers between devices, shards(): piece = lax.all_gather(dscore, EMB, axis=0, tiled=True)  48.6 us
    psum x1, blocking collectives, shards(): count = lax.psum(local_count, IMG)  24 us
    psum x1, blocking collectives, shards(): radial = lax.psum(jnp.sum(unit * dunit, axis=1), EMB)  17.2 us
    all_gather x1, waiting for transfers between devices, shards(): lax.all_gather(table, EMB, axis=1, tiled=True)  15.6 us
    dot_general x1, matrix products, shards(): jnp.dot(onehot, valid.astype(jnp.float32), preferred_element_type=jnp.flo...  9.79 us
  transfers between devices with their start and end apart: 5, of which 4 were waited for; matrix products, arithmetic and copies ran while one was open for 3% of the time, Pallas kernels for 0%

profile of v1, /device:TPU:1, one launch (start us, length us, event | category | flops | bytes accessed | tf_op | source)
XLA Modules:
  0.0 399.3 jit_solution(11736235036073792527)
XLA Ops:
  7.2 0.0 copy-start.3
  7.2 0.0 all-gather.3.cloned.1.call-start
  7.2 0.7 all-gather.3.cloned.1.call-update
  7.9 1.3 fusion.33
  9.2 9.7 %psum.77 = f32[1024]{0:T(1024)S(1)} all-reduce(f32[1024]{0:T(1024)S(1)} %fusion.33), channel_id=1, replica_groups=mesh['img_0'=4,'img_1'=2,'cls'=8,'emb_0'=2,'emb_1'=2] {'emb_0','emb_1'}, use_global_device_ids=true, to_apply=%region_1.0 | all-reduce | flops 1024 | bytes 8192 | tf_op jit(solution)/shard_map/psum | solution.py:38
  18.9 1.2 fusion.28
  20.2 1.0 copy.9
  21.2 5.2 %all-to-all-start = ((bf16[4,256,256]{1,2,0:T(8,128)(2,1)}), bf16[4,256,256]{1,2,0:T(8,128)(2,1)S(1)}, u32[]{:S(2)}, u32[]{:S(2)}) async-start(bf16[4,256,256]{1,2,0:T(8,128)(2,1)} %copy.9), calls=%async_computation | async-start | bytes 1048576 | tf_op jit(solution)/shard_map/all_to_all | solution.py:44
  26.3 0.0 all-gather.5.cloned.1.call-start
  26.3 0.0 copy-done.3
  26.3 0.6 convert_reduce_fusion
  26.9 24.0 %psum.83 = f32[]{:T(128)} all-reduce(f32[]{:T(128)} %convert_reduce_fusion), channel_id=1, replica_groups=mesh['img_0'=4,'img_1'=2,'cls'=8,'emb_0'=2,'emb_1'=2] {'img_0','img_1'}, use_global_device_ids=true, to_apply=%region_9.11 | all-reduce | flops 1 | bytes 8 | tf_op jit(solution)/shard_map/psum | solution.py:40
  51.0 0.1 dynamic_slice.9
  51.0 0.8 dynamic_slice.11
  51.8 0.8 dynamic_slice.10
  53.3 0.0 all-to-all-done
  53.3 15.6 %all-gather.3.cloned.1.call-done = bf16[2688,1024]{1,0:T(8,128)(2,1)} async-done(((bf16[2688,256]{1,0:T(8,128)(2,1)}), bf16[2688,1024]{1,0:T(8,128)(2,1)}) %all-gather.3.cloned.1.call-update) | async-done | bytes 5505040 | tf_op jit(solution)/shard_map/all_gather | solution.py:47
  68.9 0.0 copy-start.4
  68.9 4.5 %fusion = f32[256,2688]{1,0:T(8,128)S(1)} fusion(bf16[256,1024]{0,1:T(8,128)(2,1)S(1)} %bitcast.11, bf16[2688,1024]{1,0:T(8,128)(2,1)} %all-gather.3.cloned.1.call-done, f32[256]{0:T(256)S(1)} %dynamic_slice.11, f32[256]{0:T(256)S(1)} %dynamic_slice.10), kind=kOutput, calls=%fused_computation.7 | convolution fusion | flops 1410662400 | bytes 8783872 | tf_op jit(solution)/shard_map/dot_general | solution.py:45
  73.4 0.0 copy-done.4
  73.4 9.8 %fusion.12 = (bf16[256,2688]{1,0:T(8,128)(2,1)}, f32[]{:T(128)}) fusion(f32[256,2688]{1,0:T(8,128)S(1)} %fusion, f32[]{:T(128)S(6)} %div.31, f32[256]{0:T(256)S(1)} %dynamic_slice.11, s32[2688]{0:T(1024)S(1)} %iota_add_fusion, s32[256]{0:T(256)S(1)} %dynamic_slice.9, s32[2,2688]{1,0:T(2,128)S(1)} %copy-done.4, s32[256]{0:T(256)S(1)} %and_select_fusion), kind=kOutput, calls=%fused_computation.25 | convolution fusion | flops 47486720 | bytes 4164104 | tf_op jit(solution)/shard_map/dot_general | solution.py:58
  83.2 0.0 all-gather.5.cloned.1.call-update
  83.2 0.0 all-reduce.7.cloned.1.call-start
  83.3 48.6 %all-gather.5.cloned.1.call-done = bf16[1024,2688]{1,0:T(8,128)(2,1)} async-done(((bf16[256,2688]{1,0:T(8,128)(2,1)}), bf16[1024,2688]{1,0:T(8,128)(2,1)}) %all-gather.5.cloned.1.call-update) | async-done | bytes 5505040 | tf_op jit(solution)/shard_map/all_gather | solution.py:67
  131.9 5.8 %fusion.38 = f32[2688,256]{1,0:T(8,128)} fusion(bf16[1024,2688]{1,0:T(8,128)(2,1)} %all-gather.5.cloned.1.call-done, bf16[1024,256]{1,0:T(8,128)(2,1)S(1)} %fusion.28), kind=kOutput, calls=%fused_computation.64 | convolution fusion | flops 1409286144 | bytes 8781824 | tf_op jit(solution)/shard_map/dot_general | solution.py:69
  137.7 0.0 copy-start.2
  137.7 0.0 all-reduce.7.cloned.1.call-update
  137.8 0.0 copy-start
  137.8 0.0 all-reduce.5.cloned.1.call-start
  137.8 1.3 copy-done.2
  139.1 5.2 %fusion.37 = f32[1024,256]{1,0:T(8,128)} fusion(bf16[1024,2688]{1,0:T(8,128)(2,1)} %all-gather.5.cloned.1.call-done, bf16[2688,256]{1,0:T(8,128)(2,1)S(1)} %copy-done.2), kind=kOutput, calls=%fused_computation.63 | convolution fusion | flops 1409286144 | bytes 7929856 | tf_op jit(solution)/shard_map/dot_general | solution.py:68
  144.3 0.0 all-reduce.5.cloned.1.call-update
  144.3 10.1 %psum.78 = f32[]{:T(128)} all-reduce(f32[]{:T(128)} %get-tuple-element.14), channel_id=1, replica_groups=mesh['img_0'=4,'img_1'=2,'cls'=8,'emb_0'=2,'emb_1'=2] {'img_0'}, use_global_device_ids=true, to_apply=%region_3.5 | all-reduce | flops 1 | bytes 8 | tf_op jit(solution)/shard_map/psum | solution.py:21
  154.4 56.9 %all-reduce.7.cloned.1.call-done = f32[2688,256]{1,0:T(8,128)} async-done(((f32[2688,256]{1,0:T(8,128)}), f32[2688,256]{1,0:T(8,128)}) %all-reduce.7.cloned.1.call-update) | async-done | bytes 2752528 | tf_op jit(solution)/shard_map/psum | solution.py:16
  211.3 74.4 %all-reduce.5.cloned.1.call-done = f32[1024,256]{1,0:T(8,128)} async-done(((f32[1024,256]{1,0:T(8,128)}), f32[1024,256]{1,0:T(8,128)}) %all-reduce.5.cloned.1.call-update) | async-done | bytes 1048592 | tf_op jit(solution)/shard_map/psum | solution.py:72
  285.7 0.0 copy-done
  285.7 0.0 copy-start.1
  285.7 1.7 fusion.29
  287.4 61.5 %all-reduce.8 = (f32[]{:T(128)}, bf16[2688,256]{1,0:T(8,128)(2,1)}) all-reduce(f32[]{:T(128)} %psum.78, f32[2688,256]{1,0:T(8,128)} %all-reduce.7.cloned.1.call-done), channel_id=1, replica_groups=mesh['img_0'=4,'img_1'=2,'cls'=8,'emb_0'=2,'emb_1'=2] {'img_1'}, use_global_device_ids=true, to_apply=%region_4.6 | all-reduce | flops 688129 | bytes 4128776 | tf_op jit(solution)/shard_map/psum | solution.py:21
  348.9 12.4 %psum.80 = f32[]{:T(128)} all-reduce(f32[]{:T(128)} %get-tuple-element.11), channel_id=1, replica_groups=mesh['img_0'=4,'img_1'=2,'cls'=8,'emb_0'=2,'emb_1'=2] {'cls'}, use_global_device_ids=true, to_apply=%region_5.7 | all-reduce | flops 1 | bytes 8 | tf_op jit(solution)/shard_map/psum | solution.py:21
  361.3 17.2 %psum.85 = f32[1024]{0:T(1024)S(1)} all-reduce(f32[1024]{0:T(1024)S(1)} %fusion.29), channel_id=1, replica_groups=mesh['img_0'=4,'img_1'=2,'cls'=8,'emb_0'=2,'emb_1'=2] {'emb_0','emb_1'}, use_global_device_ids=true, to_apply=%region_12.14 | all-reduce | flops 1024 | bytes 8192 | tf_op jit(solution)/shard_map/psum | solution.py:73
  378.6 6.0 %psum.81 = f32[]{:T(128)} all-reduce(f32[]{:T(128)} %psum.80), channel_id=1, replica_groups=mesh['img_0'=4,'img_1'=2,'cls'=8,'emb_0'=2,'emb_1'=2] {'emb_0'}, use_global_device_ids=true, to_apply=%region_6.8 | all-reduce | flops 1 | bytes 8 | tf_op jit(solution)/shard_map/psum | solution.py:21
  384.5 0.0 copy-done.1
  384.6 1.1 fusion.32
  385.7 4.6 %psum.82 = f32[]{:T(128)} all-reduce(f32[]{:T(128)} %psum.81), channel_id=1, replica_groups=mesh['img_0'=4,'img_1'=2,'cls'=8,'emb_0'=2,'emb_1'=2] {'emb_1'}, use_global_device_ids=true, to_apply=%region_7.9 | all-reduce | flops 1 | bytes 8 | tf_op jit(solution)/shard_map/psum | solution.py:21
  (3 shorter events, 0.0 us)
Async XLA Ops:
  7.2 19.2 %copy-start.3 = (s32[1024]{0:T(1024)S(1)}, s32[1024]{0:T(1024)}, u32[]{:S(2)}) copy-start(s32[1024]{0:T(1024)} %param.11) | copy-start | bytes 12292
  7.2 61.7 %all-gather.3.cloned.1.call-start = ((), (), s32[]{:S(2)}) async-start(), calls=%async_computation.1 | async-start | bytes 6881280 | tf_op jit(solution)/shard_map/all_gather | solution.py:47
  21.2 32.1 %all-to-all-start = ((bf16[4,256,256]{1,2,0:T(8,128)(2,1)}), bf16[4,256,256]{1,2,0:T(8,128)(2,1)S(1)}, u32[]{:S(2)}, u32[]{:S(2)}) async-start(bf16[4,256,256]{1,2,0:T(8,128)(2,1)} %copy.9), calls=%async_computation | async-start | bytes 1048576 | tf_op jit(solution)/shard_map/all_to_all | solution.py:44
  26.3 105.6 %all-gather.5.cloned.1.call-start = ((), (), s32[]{:S(2)}) async-start(), calls=%async_computation.2 | async-start | bytes 6881280 | tf_op jit(solution)/shard_map/all_gather | solution.py:67
  68.9 4.5 %copy-start.4 = (s32[2,2688]{1,0:T(2,128)S(1)}, s32[2,2688]{1,0:T(2,128)}, u32[]{:S(2)}) copy-start(s32[2,2688]{1,0:T(2,128)} %param.12) | copy-start | bytes 64516
  83.2 128.1 %all-reduce.7.cloned.1.call-start = ((), (), s32[]{:S(2)}) async-start(), calls=%async_computation.4 | async-start | bytes 5505024 | tf_op jit(solution)/shard_map/psum | solution.py:16
  137.7 1.3 copy-start.2
  137.8 147.9 %copy-start = (bf16[1024,256]{1,0:T(8,128)(2,1)S(1)}, bf16[1024,256]{1,0:T(8,128)(2,1)}, u32[]{:S(2)}) copy-start(bf16[1024,256]{1,0:T(8,128)(2,1)} %param.7) | copy-start | bytes 1572868
  137.8 147.9 %all-reduce.5.cloned.1.call-start = ((), (), s32[]{:S(2)}) async-start(), calls=%async_computation.3 | async-start | bytes 2097152 | tf_op jit(solution)/shard_map/psum | solution.py:72
  285.7 98.8 %copy-start.1 = (f32[1024,256]{1,0:T(8,128)S(1)}, f32[1024,256]{1,0:T(8,128)}, u32[]{:S(2)}) copy-start(f32[1024,256]{1,0:T(8,128)} %all-reduce.5.cloned.1.call-done) | copy-start | bytes 3145732
Sparse Core Ops, SparseCore 0:
  9.8 59.0 all-gather.2
  83.4 48.5 all-gather.4
  137.9 73.3 all-reduce.6
  214.1 71.5 all-reduce.4
